TPU v7x, 32 devices: a whole 2x2x4 slice. The times are simulated.
32 devices in a mesh: blk: 8 (over y, x, core), grp: 4 (over z).
Axes of the slice: x: 2, y: 2, z: 4, core: 2. Of those that a mesh axis runs over, the one named last changes fastest.
Arguments:
- source: float32 [2048, 128], P(('blk', 'grp')), may hold values from -3 to 3
- target: float32 [2048, 128], P(('blk', 'grp')), may hold values from -3 to 3
- source_mass: float32 [2048], P(('blk', 'grp')), may hold values from 0.25 to 4
- target_mass: float32 [2048], P(('blk', 'grp')), may hold values from 0.25 to 4
Outputs:
- source_dual: float32 [2048], P(('blk', 'grp'))
- target_dual: float32 [2048], P(('blk', 'grp'))
All inputs are finite; a program needn't handle non-finite values.
Results may differ from a plain program's by a relative error of at most 0.0003.
Values sent between devices are 32-bit elements; how exact they have to be, the bound alone decides.
A program may use at most 64 MiB of HBM per device.

v0:
```python
import jax
import jax.numpy as jnp
from jax import lax
from jax.sharding import PartitionSpec as P

ITERS = 8


eps = 0.5


def combined_all(value, axis, join):
    pieces = jax.tree.map(lambda part: lax.all_gather(part, axis), value)
    head = jax.tree.map(lambda part: part[0], pieces)
    tail = jax.tree.map(lambda part: part[1:], pieces)
    subtotal, _ = lax.scan(lambda subtotal, piece: (join(subtotal, piece), None), head, tail)
    return subtotal


def partial_sums(rows, cols, col_dual, col_logmass):
    row_sq = jnp.sum(rows * rows, axis=1)
    col_sq = jnp.sum(cols * cols, axis=1)
    inner = lax.dot_general(
        rows,
        cols,
        (((1,), (1,)), ((), ())),
        precision=lax.Precision.HIGHEST,
        preferred_element_type=jnp.float32,
    )
    cost = row_sq[:, None] + col_sq[None, :] - 2.0 * inner
    score = col_logmass[None, :] + (col_dual[None, :] - cost) / eps
    top = jnp.max(score, axis=1)
    total_exp = jnp.sum(jnp.exp(score - top[:, None]), axis=1)
    return (top, total_exp)


def combine_parts(first, second):
    top = jnp.maximum(first[0], second[0])
    total_exp = first[1] * jnp.exp(first[0] - top) + second[1] * jnp.exp(second[0] - top)
    return (top, total_exp)


def spread_dual(dual):
    return lax.all_gather(dual, "grp", axis=0, tiled=True)


def finish(rows, cols, col_dual, col_logmass, count):
    top, total_exp = partial_sums(rows, cols, col_dual, col_logmass)
    top, total_exp = combined_all((top, total_exp), "blk", combine_parts)
    whole = -eps * (top + jnp.log(total_exp))
    return lax.dynamic_slice_in_dim(whole, lax.axis_index("blk") * count, count, 0)


def per_device(source, target, source_mass, target_mass):
    count = source.shape[0]
    log_source = jnp.log(source_mass)
    log_target = jnp.log(target_mass)
    row_side = (
        lax.all_gather(source, "blk", axis=0, tiled=True),
        lax.all_gather(target, "blk", axis=0, tiled=True),
        lax.all_gather(log_source, "blk", axis=0, tiled=True),
        lax.all_gather(log_target, "blk", axis=0, tiled=True),
    )
    col_side = (
        lax.all_gather(source, "grp", axis=0, tiled=True),
        lax.all_gather(target, "grp", axis=0, tiled=True),
        lax.all_gather(log_source, "grp", axis=0, tiled=True),
        lax.all_gather(log_target, "grp", axis=0, tiled=True),
    )
    source_rows, target_rows = (row_side[0], row_side[1])
    source_cols, target_cols, source_logcols, target_logcols = col_side
    target_dual = jnp.zeros((count,), jnp.float32)
    source_dual = jnp.zeros((count,), jnp.float32)
    for step in range(ITERS):
        target_spread = spread_dual(target_dual)
        source_dual = finish(source_rows, target_cols, target_spread, target_logcols, count)
        source_spread = spread_dual(source_dual)
        target_dual = finish(target_rows, source_cols, source_spread, source_logcols, count)
    return (source_dual, target_dual)


def solution(mesh):
    return jax.shard_map(
        per_device,
        mesh=mesh,
        in_specs=(
            P(("blk", "grp"), None),
            P(("blk", "grp"), None),
            P(("blk", "grp")),
            P(("blk", "grp")),
        ),
        out_specs=(P(("blk", "grp")), P(("blk", "grp"))),
        check_vma=False,
    )
```

profile of v0, /device:TPU:0, one launch (start us, length us, event | category | flops | bytes accessed | tf_op | source)
XLA Modules:
  0.0 503.1 jit_solution(10831869655434035094)
XLA Ops:
  3.3 13.5 %all-reduce = f32[256]{0:T(256)S(1)} all-reduce(f32[256]{0:T(256)S(1)} %log_dynamic-update-slice_fusion.1), channel_id=1, replica_groups=mesh['blk'=8,'grp'=4] {'grp'}, use_global_device_ids=true, to_apply=%add | all-reduce | flops 256 | bytes 2048
  16.7 9.5 %all_gather.258 = f32[512,128]{1,0:T(8,128)S(1)} all-gather(f32[64,128]{1,0:T(8,128)} %param.36), channel_id=1, replica_groups=mesh['blk'=8,'grp'=4] {'blk'}, dimensions={0}, use_global_device_ids=true | all-gather | bytes 294912 | tf_op jit(solution)/shard_map/all_gather | solution.py:59
  27.0 13.4 %all_gather.259 = f32[256,128]{1,0:T(8,128)S(1)} all-gather(f32[64,128]{1,0:T(8,128)S(1)} %copy-done), channel_id=1, replica_groups=mesh['blk'=8,'grp'=4] {'grp'}, dimensions={0}, use_global_device_ids=true | all-gather | bytes 163840 | tf_op jit(solution)/shard_map/all_gather | solution.py:66
  40.5 0.7 fusion.2
  41.4 8.7 %all-gather.33 = f32[8,1,512]{2,1,0:T(1,128)S(1)} all-gather(f32[1,1,512]{2,1,0:T(1,128)S(1)} %bitcast.388), channel_id=3, replica_groups=mesh['blk'=8,'grp'=4] {'blk'}, dimensions={0}, use_global_device_ids=true | all-gather | bytes 18432 | tf_op jit(solution)/shard_map/all_gather | solution.py:13
  50.7 8.1 %all-gather.32 = f32[8,1,512]{2,1,0:T(1,128)S(1)} all-gather(f32[1,1,512]{2,1,0:T(1,128)S(1)} %bitcast.372), channel_id=2, replica_groups=mesh['blk'=8,'grp'=4] {'blk'}, dimensions={0}, use_global_device_ids=true | all-gather | bytes 18432 | tf_op jit(solution)/shard_map/all_gather | solution.py:13
  61.4 8.5 %all-reduce.17 = (f32[256]{0:T(256)S(1)}, f32[256]{0:T(256)S(1)}) all-reduce(f32[256]{0:T(256)S(1)} %dynamic-slice_dynamic-update-slice_fusion.13, f32[256]{0:T(256)S(1)} %log_dynamic-update-slice_fusion), channel_id=1, replica_groups=mesh['blk'=8,'grp'=4] {'grp'}, use_global_device_ids=true, to_apply=%add.2 | all-reduce | flops 512 | bytes 4096
  69.9 9.1 %all_gather.265 = f32[512,128]{1,0:T(8,128)S(1)} all-gather(f32[64,128]{1,0:T(8,128)S(1)} %copy-done), channel_id=1, replica_groups=mesh['blk'=8,'grp'=4] {'blk'}, dimensions={0}, use_global_device_ids=true | all-gather | bytes 294912 | tf_op jit(solution)/shard_map/all_gather | solution.py:60
  79.7 13.3 %all_gather.266 = f32[256,128]{1,0:T(8,128)S(1)} all-gather(f32[64,128]{1,0:T(8,128)S(1)} %copy-done.1), channel_id=1, replica_groups=mesh['blk'=8,'grp'=4] {'grp'}, dimensions={0}, use_global_device_ids=true | all-gather | bytes 163840 | tf_op jit(solution)/shard_map/all_gather | solution.py:65
  93.2 0.7 fusion.3
  94.1 8.2 %all-gather.35 = f32[8,1,512]{2,1,0:T(1,128)S(1)} all-gather(f32[1,1,512]{2,1,0:T(1,128)S(1)} %bitcast.375), channel_id=5, replica_groups=mesh['blk'=8,'grp'=4] {'blk'}, dimensions={0}, use_global_device_ids=true | all-gather | bytes 18432 | tf_op jit(solution)/shard_map/all_gather | solution.py:13
  102.8 8.7 %all-gather.34 = f32[8,1,512]{2,1,0:T(1,128)S(1)} all-gather(f32[1,1,512]{2,1,0:T(1,128)S(1)} %bitcast.371), channel_id=4, replica_groups=mesh['blk'=8,'grp'=4] {'blk'}, dimensions={0}, use_global_device_ids=true | all-gather | bytes 18432 | tf_op jit(solution)/shard_map/all_gather | solution.py:13
  111.5 0.7 slice-done.1
  112.7 10.2 %all-reduce.3 = f32[256]{0:T(256)S(1)} all-reduce(f32[256]{0:T(256)S(1)} %dynamic-slice_dynamic-update-slice_fusion.12), channel_id=1, replica_groups=mesh['blk'=8,'grp'=4] {'grp'}, use_global_device_ids=true, to_apply=%add.3 | all-reduce | flops 256 | bytes 2048
  123.3 8.2 %all-gather.37 = f32[8,1,512]{2,1,0:T(1,128)S(1)} all-gather(f32[1,1,512]{2,1,0:T(1,128)S(1)} %bitcast.376), channel_id=7, replica_groups=mesh['blk'=8,'grp'=4] {'blk'}, dimensions={0}, use_global_device_ids=true | all-gather | bytes 18432 | tf_op jit(solution)/shard_map/all_gather | solution.py:13
  131.5 8.7 %all-gather.36 = f32[8,1,512]{2,1,0:T(1,128)S(1)} all-gather(f32[1,1,512]{2,1,0:T(1,128)S(1)} %bitcast.359), channel_id=6, replica_groups=mesh['blk'=8,'grp'=4] {'blk'}, dimensions={0}, use_global_device_ids=true | all-gather | bytes 18432 | tf_op jit(solution)/shard_map/all_gather | solution.py:13
  140.2 0.7 slice-done.3
  141.4 8.5 %all-reduce.4 = f32[256]{0:T(256)S(1)} all-reduce(f32[256]{0:T(256)S(1)} %dynamic-slice_dynamic-update-slice_fusion.11), channel_id=1, replica_groups=mesh['blk'=8,'grp'=4] {'grp'}, use_global_device_ids=true, to_apply=%add.4 | all-reduce | flops 256 | bytes 2048
  150.2 8.2 %all-gather.39 = f32[8,1,512]{2,1,0:T(1,128)S(1)} all-gather(f32[1,1,512]{2,1,0:T(1,128)S(1)} %bitcast.377), channel_id=9, replica_groups=mesh['blk'=8,'grp'=4] {'blk'}, dimensions={0}, use_global_device_ids=true | all-gather | bytes 18432 | tf_op jit(solution)/shard_map/all_gather | solution.py:13
  158.4 8.7 %all-gather.38 = f32[8,1,512]{2,1,0:T(1,128)S(1)} all-gather(f32[1,1,512]{2,1,0:T(1,128)S(1)} %bitcast.360), channel_id=8, replica_groups=mesh['blk'=8,'grp'=4] {'blk'}, dimensions={0}, use_global_device_ids=true | all-gather | bytes 18432 | tf_op jit(solution)/shard_map/all_gather | solution.py:13
  167.1 0.7 slice-done.4
  168.4 10.2 %all-reduce.5 = f32[256]{0:T(256)S(1)} all-reduce(f32[256]{0:T(256)S(1)} %dynamic-slice_dynamic-update-slice_fusion.10), channel_id=1, replica_groups=mesh['blk'=8,'grp'=4] {'grp'}, use_global_device_ids=true, to_apply=%add.5 | all-reduce | flops 256 | bytes 2048
  178.9 8.2 %all-gather.41 = f32[8,1,512]{2,1,0:T(1,128)S(1)} all-gather(f32[1,1,512]{2,1,0:T(1,128)S(1)} %bitcast.378), channel_id=11, replica_groups=mesh['blk'=8,'grp'=4] {'blk'}, dimensions={0}, use_global_device_ids=true | all-gather | bytes 18432 | tf_op jit(solution)/shard_map/all_gather | solution.py:13
  187.1 8.7 %all-gather.40 = f32[8,1,512]{2,1,0:T(1,128)S(1)} all-gather(f32[1,1,512]{2,1,0:T(1,128)S(1)} %bitcast.361), channel_id=10, replica_groups=mesh['blk'=8,'grp'=4] {'blk'}, dimensions={0}, use_global_device_ids=true | all-gather | bytes 18432 | tf_op jit(solution)/shard_map/all_gather | solution.py:13
  195.8 0.7 slice-done.5
  197.0 8.5 %all-reduce.6 = f32[256]{0:T(256)S(1)} all-reduce(f32[256]{0:T(256)S(1)} %dynamic-slice_dynamic-update-slice_fusion.9), channel_id=1, replica_groups=mesh['blk'=8,'grp'=4] {'grp'}, use_global_device_ids=true, to_apply=%add.6 | all-reduce | flops 256 | bytes 2048
  205.9 8.2 %all-gather.43 = f32[8,1,512]{2,1,0:T(1,128)S(1)} all-gather(f32[1,1,512]{2,1,0:T(1,128)S(1)} %bitcast.379), channel_id=13, replica_groups=mesh['blk'=8,'grp'=4] {'blk'}, dimensions={0}, use_global_device_ids=true | all-gather | bytes 18432 | tf_op jit(solution)/shard_map/all_gather | solution.py:13
  214.0 8.7 %all-gather.42 = f32[8,1,512]{2,1,0:T(1,128)S(1)} all-gather(f32[1,1,512]{2,1,0:T(1,128)S(1)} %bitcast.362), channel_id=12, replica_groups=mesh['blk'=8,'grp'=4] {'blk'}, dimensions={0}, use_global_device_ids=true | all-gather | bytes 18432 | tf_op jit(solution)/shard_map/all_gather | solution.py:13
  222.8 0.7 slice-done.6
  224.0 10.2 %all-reduce.7 = f32[256]{0:T(256)S(1)} all-reduce(f32[256]{0:T(256)S(1)} %dynamic-slice_dynamic-update-slice_fusion.8), channel_id=1, replica_groups=mesh['blk'=8,'grp'=4] {'grp'}, use_global_device_ids=true, to_apply=%add.7 | all-reduce | flops 256 | bytes 2048
  234.5 8.2 %all-gather.45 = f32[8,1,512]{2,1,0:T(1,128)S(1)} all-gather(f32[1,1,512]{2,1,0:T(1,128)S(1)} %bitcast.380), channel_id=15, replica_groups=mesh['blk'=8,'grp'=4] {'blk'}, dimensions={0}, use_global_device_ids=true | all-gather | bytes 18432 | tf_op jit(solution)/shard_map/all_gather | solution.py:13
  242.7 8.7 %all-gather.44 = f32[8,1,512]{2,1,0:T(1,128)S(1)} all-gather(f32[1,1,512]{2,1,0:T(1,128)S(1)} %bitcast.363), channel_id=14, replica_groups=mesh['blk'=8,'grp'=4] {'blk'}, dimensions={0}, use_global_device_ids=true | all-gather | bytes 18432 | tf_op jit(solution)/shard_map/all_gather | solution.py:13
  251.4 0.7 slice-done.7
  252.7 8.7 %all-reduce.8 = f32[256]{0:T(256)S(1)} all-reduce(f32[256]{0:T(256)S(1)} %dynamic-slice_dynamic-update-slice_fusion.7), channel_id=1, replica_groups=mesh['blk'=8,'grp'=4] {'grp'}, use_global_device_ids=true, to_apply=%add.8 | all-reduce | flops 256 | bytes 2048
  261.7 8.2 %all-gather.47 = f32[8,1,512]{2,1,0:T(1,128)S(1)} all-gather(f32[1,1,512]{2,1,0:T(1,128)S(1)} %bitcast.381), channel_id=17, replica_groups=mesh['blk'=8,'grp'=4] {'blk'}, dimensions={0}, use_global_device_ids=true | all-gather | bytes 18432 | tf_op jit(solution)/shard_map/all_gather | solution.py:13
  269.8 8.7 %all-gather.46 = f32[8,1,512]{2,1,0:T(1,128)S(1)} all-gather(f32[1,1,512]{2,1,0:T(1,128)S(1)} %bitcast.364), channel_id=16, replica_groups=mesh['blk'=8,'grp'=4] {'blk'}, dimensions={0}, use_global_device_ids=true | all-gather | bytes 18432 | tf_op jit(solution)/shard_map/all_gather | solution.py:13
  278.6 0.7 slice-done.8
  279.8 10.2 %all-reduce.9 = f32[256]{0:T(256)S(1)} all-reduce(f32[256]{0:T(256)S(1)} %dynamic-slice_dynamic-update-slice_fusion.6), channel_id=1, replica_groups=mesh['blk'=8,'grp'=4] {'grp'}, use_global_device_ids=true, to_apply=%add.9 | all-reduce | flops 256 | bytes 2048
  290.4 8.2 %all-gather.49 = f32[8,1,512]{2,1,0:T(1,128)S(1)} all-gather(f32[1,1,512]{2,1,0:T(1,128)S(1)} %bitcast.382), channel_id=19, replica_groups=mesh['blk'=8,'grp'=4] {'blk'}, dimensions={0}, use_global_device_ids=true | all-gather | bytes 18432 | tf_op jit(solution)/shard_map/all_gather | solution.py:13
  298.5 8.7 %all-gather.48 = f32[8,1,512]{2,1,0:T(1,128)S(1)} all-gather(f32[1,1,512]{2,1,0:T(1,128)S(1)} %bitcast.365), channel_id=18, replica_groups=mesh['blk'=8,'grp'=4] {'blk'}, dimensions={0}, use_global_device_ids=true | all-gather | bytes 18432 | tf_op jit(solution)/shard_map/all_gather | solution.py:13
  308.5 8.5 %all-reduce.10 = f32[256]{0:T(256)S(1)} all-reduce(f32[256]{0:T(256)S(1)} %dynamic-slice_dynamic-update-slice_fusion.5), channel_id=1, replica_groups=mesh['blk'=8,'grp'=4] {'grp'}, use_global_device_ids=true, to_apply=%add.10 | all-reduce | flops 256 | bytes 2048
  317.3 8.2 %all-gather.51 = f32[8,1,512]{2,1,0:T(1,128)S(1)} all-gather(f32[1,1,512]{2,1,0:T(1,128)S(1)} %bitcast.383), channel_id=21, replica_groups=mesh['blk'=8,'grp'=4] {'blk'}, dimensions={0}, use_global_device_ids=true | all-gather | bytes 18432 | tf_op jit(solution)/shard_map/all_gather | solution.py:13
  325.5 8.7 %all-gather.50 = f32[8,1,512]{2,1,0:T(1,128)S(1)} all-gather(f32[1,1,512]{2,1,0:T(1,128)S(1)} %bitcast.366), channel_id=20, replica_groups=mesh['blk'=8,'grp'=4] {'blk'}, dimensions={0}, use_global_device_ids=true | all-gather | bytes 18432 | tf_op jit(solution)/shard_map/all_gather | solution.py:13
  334.2 0.7 slice-done.10
  335.4 10.2 %all-reduce.11 = f32[256]{0:T(256)S(1)} all-reduce(f32[256]{0:T(256)S(1)} %dynamic-slice_dynamic-update-slice_fusion.4), channel_id=1, replica_groups=mesh['blk'=8,'grp'=4] {'grp'}, use_global_device_ids=true, to_apply=%add.11 | all-reduce | flops 256 | bytes 2048
  346.0 8.2 %all-gather.53 = f32[8,1,512]{2,1,0:T(1,128)S(1)} all-gather(f32[1,1,512]{2,1,0:T(1,128)S(1)} %bitcast.384), channel_id=23, replica_groups=mesh['blk'=8,'grp'=4] {'blk'}, dimensions={0}, use_global_device_ids=true | all-gather | bytes 18432 | tf_op jit(solution)/shard_map/all_gather | solution.py:13
  354.2 8.7 %all-gather.52 = f32[8,1,512]{2,1,0:T(1,128)S(1)} all-gather(f32[1,1,512]{2,1,0:T(1,128)S(1)} %bitcast.367), channel_id=22, replica_groups=mesh['blk'=8,'grp'=4] {'blk'}, dimensions={0}, use_global_device_ids=true | all-gather | bytes 18432 | tf_op jit(solution)/shard_map/all_gather | solution.py:13
  362.9 0.7 slice-done.11
  364.1 8.5 %all-reduce.12 = f32[256]{0:T(256)S(1)} all-reduce(f32[256]{0:T(256)S(1)} %dynamic-slice_dynamic-update-slice_fusion.3), channel_id=1, replica_groups=mesh['blk'=8,'grp'=4] {'grp'}, use_global_device_ids=true, to_apply=%add.12 | all-reduce | flops 256 | bytes 2048
  372.9 8.2 %all-gather.55 = f32[8,1,512]{2,1,0:T(1,128)S(1)} all-gather(f32[1,1,512]{2,1,0:T(1,128)S(1)} %bitcast.385), channel_id=25, replica_groups=mesh['blk'=8,'grp'=4] {'blk'}, dimensions={0}, use_global_device_ids=true | all-gather | bytes 18432 | tf_op jit(solution)/shard_map/all_gather | solution.py:13
  381.1 8.7 %all-gather.54 = f32[8,1,512]{2,1,0:T(1,128)S(1)} all-gather(f32[1,1,512]{2,1,0:T(1,128)S(1)} %bitcast.368), channel_id=24, replica_groups=mesh['blk'=8,'grp'=4] {'blk'}, dimensions={0}, use_global_device_ids=true | all-gather | bytes 18432 | tf_op jit(solution)/shard_map/all_gather | solution.py:13
  389.8 0.7 slice-done.12
  391.0 10.2 %all-reduce.13 = f32[256]{0:T(256)S(1)} all-reduce(f32[256]{0:T(256)S(1)} %dynamic-slice_dynamic-update-slice_fusion.2), channel_id=1, replica_groups=mesh['blk'=8,'grp'=4] {'grp'}, use_global_device_ids=true, to_apply=%add.13 | all-reduce | flops 256 | bytes 2048
  401.6 8.2 %all-gather.57 = f32[8,1,512]{2,1,0:T(1,128)S(1)} all-gather(f32[1,1,512]{2,1,0:T(1,128)S(1)} %bitcast.386), channel_id=27, replica_groups=mesh['blk'=8,'grp'=4] {'blk'}, dimensions={0}, use_global_device_ids=true | all-gather | bytes 18432 | tf_op jit(solution)/shard_map/all_gather | solution.py:13
  409.8 8.7 %all-gather.56 = f32[8,1,512]{2,1,0:T(1,128)S(1)} all-gather(f32[1,1,512]{2,1,0:T(1,128)S(1)} %bitcast.369), channel_id=26, replica_groups=mesh['blk'=8,'grp'=4] {'blk'}, dimensions={0}, use_global_device_ids=true | all-gather | bytes 18432 | tf_op jit(solution)/shard_map/all_gather | solution.py:13
  419.7 8.5 %all-reduce.14 = f32[256]{0:T(256)S(1)} all-reduce(f32[256]{0:T(256)S(1)} %dynamic-slice_dynamic-update-slice_fusion.1), channel_id=1, replica_groups=mesh['blk'=8,'grp'=4] {'grp'}, use_global_device_ids=true, to_apply=%add.14 | all-reduce | flops 256 | bytes 2048
  428.6 8.2 %all-gather.59 = f32[8,1,512]{2,1,0:T(1,128)S(1)} all-gather(f32[1,1,512]{2,1,0:T(1,128)S(1)} %bitcast.387), channel_id=29, replica_groups=mesh['blk'=8,'grp'=4] {'blk'}, dimensions={0}, use_global_device_ids=true | all-gather | bytes 18432 | tf_op jit(solution)/shard_map/all_gather | solution.py:13
  436.7 8.7 %all-gather.58 = f32[8,1,512]{2,1,0:T(1,128)S(1)} all-gather(f32[1,1,512]{2,1,0:T(1,128)S(1)} %bitcast.370), channel_id=28, replica_groups=mesh['blk'=8,'grp'=4] {'blk'}, dimensions={0}, use_global_device_ids=true | all-gather | bytes 18432 | tf_op jit(solution)/shard_map/all_gather | solution.py:13
  446.7 10.2 %all-reduce.15 = f32[256]{0:T(256)S(1)} all-reduce(f32[256]{0:T(256)S(1)} %dynamic-slice_dynamic-update-slice_fusion), channel_id=1, replica_groups=mesh['blk'=8,'grp'=4] {'grp'}, use_global_device_ids=true, to_apply=%add.15 | all-reduce | flops 256 | bytes 2048
  457.2 8.2 %all-gather.61 = f32[8,1,512]{2,1,0:T(1,128)S(1)} all-gather(f32[1,1,512]{2,1,0:T(1,128)S(1)} %bitcast.373), channel_id=31, replica_groups=mesh['blk'=8,'grp'=4] {'blk'}, dimensions={0}, use_global_device_ids=true | all-gather | bytes 18432 | tf_op jit(solution)/shard_map/all_gather | solution.py:13
  465.4 8.7 %all-gather.60 = f32[8,1,512]{2,1,0:T(1,128)S(1)} all-gather(f32[1,1,512]{2,1,0:T(1,128)S(1)} %bitcast.357), channel_id=30, replica_groups=mesh['blk'=8,'grp'=4] {'blk'}, dimensions={0}, use_global_device_ids=true | all-gather | bytes 18432 | tf_op jit(solution)/shard_map/all_gather | solution.py:13
  475.8 8.5 %all-reduce.16 = f32[256]{0:T(256)S(1)} all-reduce(f32[256]{0:T(256)S(1)} %get-tuple-element.676), channel_id=1, replica_groups=mesh['blk'=8,'grp'=4] {'grp'}, use_global_device_ids=true, to_apply=%add.16 | all-reduce | flops 256 | bytes 2048
  484.6 8.2 %all-gather.63 = f32[8,1,512]{2,1,0:T(1,128)S(1)} all-gather(f32[1,1,512]{2,1,0:T(1,128)S(1)} %bitcast.374), channel_id=33, replica_groups=mesh['blk'=8,'grp'=4] {'blk'}, dimensions={0}, use_global_device_ids=true | all-gather | bytes 18432 | tf_op jit(solution)/shard_map/all_gather | solution.py:13
  492.8 8.7 %all-gather.62 = f32[8,1,512]{2,1,0:T(1,128)S(1)} all-gather(f32[1,1,512]{2,1,0:T(1,128)S(1)} %bitcast.358), channel_id=32, replica_groups=mesh['blk'=8,'grp'=4] {'blk'}, dimensions={0}, use_global_device_ids=true | all-gather | bytes 18432 | tf_op jit(solution)/shard_map/all_gather | solution.py:13
  (473 shorter events, 28.6 us)
Async XLA Ops:
  0.6 0.7 copy-start.21
  2.5 0.7 copy-start.19
  26.2 0.8 copy-start
  50.1 0.6 copy-start.2
  58.8 0.6 copy-start.4
  59.4 0.7 slice-start.2
  59.4 0.7 slice-start
  60.6 0.7 copy-start.20
  78.9 0.8 copy-start.1
  102.2 0.6 copy-start.3
  111.5 0.7 slice-start.1
  131.5 8.7 %copy-start.5 = (f32[8,1,512]{2,1,0:T(1,128)}, f32[8,1,512]{2,1,0:T(1,128)S(1)}, u32[]{:S(2)}) copy-start(f32[8,1,512]{2,1,0:T(1,128)S(1)} %all-gather.37) | copy-start | bytes 49156
  140.2 0.7 slice-start.3
  158.4 8.7 %copy-start.6 = (f32[8,1,512]{2,1,0:T(1,128)}, f32[8,1,512]{2,1,0:T(1,128)S(1)}, u32[]{:S(2)}) copy-start(f32[8,1,512]{2,1,0:T(1,128)S(1)} %all-gather.39) | copy-start | bytes 49156
  167.1 0.7 slice-start.4
  187.1 8.7 %copy-start.7 = (f32[8,1,512]{2,1,0:T(1,128)}, f32[8,1,512]{2,1,0:T(1,128)S(1)}, u32[]{:S(2)}) copy-start(f32[8,1,512]{2,1,0:T(1,128)S(1)} %all-gather.41) | copy-start | bytes 49156
  195.8 0.7 slice-start.5
  214.0 8.7 %copy-start.8 = (f32[8,1,512]{2,1,0:T(1,128)}, f32[8,1,512]{2,1,0:T(1,128)S(1)}, u32[]{:S(2)}) copy-start(f32[8,1,512]{2,1,0:T(1,128)S(1)} %all-gather.43) | copy-start | bytes 49156
  222.7 0.7 slice-start.6
  242.7 8.7 %copy-start.9 = (f32[8,1,512]{2,1,0:T(1,128)}, f32[8,1,512]{2,1,0:T(1,128)S(1)}, u32[]{:S(2)}) copy-start(f32[8,1,512]{2,1,0:T(1,128)S(1)} %all-gather.45) | copy-start | bytes 49156
  251.4 0.7 slice-start.7
  269.8 8.7 %copy-start.10 = (f32[8,1,512]{2,1,0:T(1,128)}, f32[8,1,512]{2,1,0:T(1,128)S(1)}, u32[]{:S(2)}) copy-start(f32[8,1,512]{2,1,0:T(1,128)S(1)} %all-gather.47) | copy-start | bytes 49156
  278.6 0.7 slice-start.8
  298.5 8.7 %copy-start.11 = (f32[8,1,512]{2,1,0:T(1,128)}, f32[8,1,512]{2,1,0:T(1,128)S(1)}, u32[]{:S(2)}) copy-start(f32[8,1,512]{2,1,0:T(1,128)S(1)} %all-gather.49) | copy-start | bytes 49156
  307.2 0.7 slice-start.9
  325.5 8.7 %copy-start.12 = (f32[8,1,512]{2,1,0:T(1,128)}, f32[8,1,512]{2,1,0:T(1,128)S(1)}, u32[]{:S(2)}) copy-start(f32[8,1,512]{2,1,0:T(1,128)S(1)} %all-gather.51) | copy-start | bytes 49156
  334.2 0.7 slice-start.10
  354.1 8.7 %copy-start.13 = (f32[8,1,512]{2,1,0:T(1,128)}, f32[8,1,512]{2,1,0:T(1,128)S(1)}, u32[]{:S(2)}) copy-start(f32[8,1,512]{2,1,0:T(1,128)S(1)} %all-gather.53) | copy-start | bytes 49156
  362.9 0.7 slice-start.11
  381.1 8.7 %copy-start.14 = (f32[8,1,512]{2,1,0:T(1,128)}, f32[8,1,512]{2,1,0:T(1,128)S(1)}, u32[]{:S(2)}) copy-start(f32[8,1,512]{2,1,0:T(1,128)S(1)} %all-gather.55) | copy-start | bytes 49156
  389.8 0.7 slice-start.12
  409.8 8.7 %copy-start.15 = (f32[8,1,512]{2,1,0:T(1,128)}, f32[8,1,512]{2,1,0:T(1,128)S(1)}, u32[]{:S(2)}) copy-start(f32[8,1,512]{2,1,0:T(1,128)S(1)} %all-gather.57) | copy-start | bytes 49156
  418.5 0.7 slice-start.13
  436.7 8.7 %copy-start.16 = (f32[8,1,512]{2,1,0:T(1,128)}, f32[8,1,512]{2,1,0:T(1,128)S(1)}, u32[]{:S(2)}) copy-start(f32[8,1,512]{2,1,0:T(1,128)S(1)} %all-gather.59) | copy-start | bytes 49156
  445.4 0.7 slice-start.14
  465.4 8.7 %copy-start.17 = (f32[8,1,512]{2,1,0:T(1,128)}, f32[8,1,512]{2,1,0:T(1,128)S(1)}, u32[]{:S(2)}) copy-start(f32[8,1,512]{2,1,0:T(1,128)S(1)} %all-gather.61) | copy-start | bytes 49156
  474.1 0.7 slice-start.15
  492.8 8.7 %copy-start.18 = (f32[8,1,512]{2,1,0:T(1,128)}, f32[8,1,512]{2,1,0:T(1,128)S(1)}, u32[]{:S(2)}) copy-start(f32[8,1,512]{2,1,0:T(1,128)S(1)} %all-gather.63) | copy-start | bytes 49156
  501.5 0.7 slice-start.16
where the time goes:
time: 505 us; the launch traced here: 503 us
  blocking collectives  468 us (93%)
  local copies, waits for them, and re-layouts  21.5 us (4%)
  other arithmetic  8.35 us (2%)
    all_gather x32, blocking collectives, combined_all(): pieces = jax.tree.map(lambda part: lax.all_gather(part, axis), value)  269 us
    unnamed x16, blocking collectives  153 us
    all_gather x1, blocking collectives, per_device(): lax.all_gather(target, 'grp', axis=0, tiled=True)  13.4 us
    all_gather x1, blocking collectives, per_device(): lax.all_gather(source, 'grp', axis=0, tiled=True)  13.3 us
    slice x49, local copies, waits for them, and re-layouts, combined_all(): head = jax.tree.map(lambda part: part[0], pieces)  10.8 us

commit v1 on v0

v1 whole, which is shorter than its diff:
```python
import functools
import math

import jax
import jax.numpy as jnp
from jax import lax
from jax.experimental import pallas as pl
from jax.experimental.pallas import tpu as pltpu
from jax.sharding import PartitionSpec as P

ITERS = 8
eps = 0.5
LOG2E = math.log2(math.e)
ALPHA = LOG2E / eps
LANES = 128
SUB = 8
MESH = pl.DeviceIdType.MESH
BUDGET = 36 * 2**20


def exp2(x):
    return jnp.exp2(x)


def log2(x):
    return jnp.log(x) * LOG2E


def lse_blocks(pairs):
    top = functools.reduce(jnp.maximum, [m for m, _ in pairs])
    if len(pairs) == 1:
        return pairs[0]
    return top, sum(s * exp2(m - top) for m, s in pairs)


def kernel(blk_n, grp_n, part, count, src_ref, tgt_ref, smass_ref, tmass_ref, out_ref,
           src_all, tgt_all, spack, tpack, cost, tcat, u, v, loga, logb, part_lse,
           s_send, s_recv, t_send, t_recv, x_send, x_recv):
    n_dev = blk_n * grp_n
    rep = LANES // count
    chunks = n_dev // rep
    quads = blk_n // part
    t_dev = quads * grp_n
    nj = t_dev * count
    b, g = lax.axis_index("blk"), lax.axis_index("grp")
    me = b * grp_n + g
    q, p = b // part, b % part
    mine_t = q * grp_n + g

    barrier = pltpu.get_barrier_semaphore()

    def greet(step, _):
        other = lax.rem(me + step, n_dev)
        pl.semaphore_signal(barrier, inc=1, device_id=(other // grp_n, other % grp_n), device_id_type=MESH)
        return 0

    lax.fori_loop(1, n_dev, greet, 0)

    lane = lax.broadcasted_iota(jnp.int32, (1, LANES), 1)
    here = lane // count == me % rep

    def pack(ref, mass_ref, out, scale):
        out[0:count, :] = ref[...] * scale
        row = log2(mass_ref[...])
        row = jnp.where(here, jnp.concatenate([row] * rep, axis=1), 0.0)
        out[count : count + SUB, :] = jnp.broadcast_to(row, (SUB, LANES))

    pack(src_ref, smass_ref, spack, 2.0 * ALPHA)
    pack(tgt_ref, tmass_ref, tpack, 1.0)
    src_all[pl.ds(me, 1)] = spack[...][None]
    tgt_all[pl.ds(mine_t, 1)] = tpack[...][None]
    pl.semaphore_wait(barrier, n_dev - 1)

    def tgt_copy(slot, r, sem_slot):
        return pltpu.make_async_remote_copy(
            src_ref=tpack, dst_ref=tgt_all.at[slot],
            send_sem=t_send.at[r], recv_sem=t_recv.at[sem_slot],
            device_id=((r // grp_n) * part + p, r % grp_n), device_id_type=MESH)

    def src_copy(slot, d):
        return pltpu.make_async_remote_copy(
            src_ref=spack, dst_ref=src_all.at[slot],
            send_sem=s_send.at[d], recv_sem=s_recv.at[slot],
            device_id=(d // grp_n, d % grp_n), device_id_type=MESH)

    def send_t(step, _):
        r = lax.rem(mine_t + step, t_dev)
        tgt_copy(mine_t, r, mine_t).start()
        return 0

    def send_s(step, _):
        src_copy(me, lax.rem(me + step, n_dev)).start()
        return 0

    def wait_t(step, _):
        r = lax.rem(mine_t + step, t_dev)
        tgt_copy(mine_t, r, mine_t).wait_send()
        tgt_copy(r, r, r).wait_recv()
        return 0

    def wait_s(step, _):
        d = lax.rem(me + step, n_dev)
        src_copy(me, d).wait_send()
        src_copy(d, d).wait_recv()
        return 0

    lax.fori_loop(1, t_dev, send_t, 0)
    lax.fori_loop(1, n_dev, send_s, 0)
    lax.fori_loop(1, t_dev, wait_t, 0)

    eye = (lax.broadcasted_iota(jnp.int32, (count, LANES), 1) % count
           == lax.broadcasted_iota(jnp.int32, (count, LANES), 0))
    for r in range(t_dev):
        rows = slice(r * count, (r + 1) * count)
        block = tgt_all[r, 0:count, :]
        tcat[rows, :] = block
        mass = jnp.sum(jnp.where(eye, tgt_all[r, count : count + 1, :], 0.0), axis=1, keepdims=True)
        square = jnp.sum(block * block, axis=1, keepdims=True)
        logb[rows, :] = jnp.broadcast_to(mass, (count, LANES))
        u[rows, :] = jnp.broadcast_to(mass - ALPHA * square, (count, LANES))

    lax.fori_loop(1, n_dev, wait_s, 0)

    def make_cost(k, _):
        pieces = [src_all[k * rep + i, 0:count, :] for i in range(rep)]
        masses = sum(src_all[k * rep + i, count : count + 1, :] for i in range(rep))
        loga[pl.ds(k, 1), :] = masses
        cost[k] = lax.dot_general(
            tcat[...], jnp.concatenate(pieces, axis=0), (((1,), (1,)), ((), ())),
            precision=lax.Precision.HIGHEST, preferred_element_type=jnp.float32)
        return 0

    lax.fori_loop(0, chunks, make_cost, 0)

    rows_at_once = min(nj, 128)

    def source_chunk(slot, k):
        pairs = []
        for r in range(0, nj, rows_at_once):
            x = cost[k, r : r + rows_at_once, :] + u[r : r + rows_at_once, :]
            x = x.reshape(rows_at_once // SUB, SUB, LANES)
            m = jnp.max(x, axis=0)
            pairs.append((m, jnp.sum(exp2(x - m[None]), axis=0)))
        m, s = lse_blocks(pairs)
        top = jnp.max(m, axis=0, keepdims=True)
        total = jnp.sum(s * exp2(m - top), axis=0, keepdims=True)
        part_lse[slot, p, pl.ds(k, 1), :] = top + log2(total)

    groups = math.gcd(nj // SUB, 8)

    def target_rows(i, _):
        for h in range(groups):
            rows = pl.ds(pl.multiple_of((i * groups + h) * SUB, SUB), SUB)
            pairs = []
            for k0 in range(0, chunks, 16):
                x = [cost[k, rows, :] + v[k : k + 1, :] for k in range(k0, min(k0 + 16, chunks))]
                m = functools.reduce(jnp.maximum, x)
                pairs.append((m, sum(exp2(y - m) for y in x)))
            m, s = lse_blocks(pairs)
            top = jnp.max(m, axis=1, keepdims=True)
            total = jnp.sum(s * exp2(m - top), axis=1, keepdims=True)
            u[rows, :] = logb[rows, :] - (top + log2(total))
        return 0

    def swap(slot, writer, other, sem_at):
        return pltpu.make_async_remote_copy(
            src_ref=part_lse.at[slot, p], dst_ref=part_lse.at[slot, writer],
            send_sem=x_send.at[slot, other], recv_sem=x_recv.at[slot, sem_at],
            device_id=(q * part + other, g), device_id_type=MESH)

    def iteration(t, _):
        slot = lax.rem(t, 2)

        def one(k, _):
            source_chunk(slot, k)
            return 0

        lax.fori_loop(0, chunks, one, 0)
        for step in range(1, part):
            other = lax.rem(p + step, part)
            swap(slot, p, other, p).start()
        for step in range(1, part):
            other = lax.rem(p + step, part)
            swap(slot, p, other, p).wait_send()
            swap(slot, other, other, other).wait_recv()
        parts = [part_lse[slot, i] for i in range(part)]
        top = functools.reduce(jnp.maximum, parts)
        v[...] = loga[...] - (top + log2(sum(exp2(y - top) for y in parts)))
        lax.fori_loop(0, nj // (SUB * groups), target_rows, 0)
        return 0

    lax.fori_loop(0, ITERS, iteration, 0)

    def to_lanes(column):
        return jnp.sum(jnp.where(eye, column, 0.0), axis=0, keepdims=True)

    src = src_ref[...]
    row = pl.ds(me // rep, 1)
    lse_s = loga[row, :] - v[row, :]
    first = to_lanes(jnp.sum(src * src, axis=1, keepdims=True)) - (1.0 / ALPHA) * lse_s
    tgt = tgt_ref[...]
    own = pl.ds(pl.multiple_of(mine_t * count, count), count)
    lse_t = logb[own, :] - u[own, :]
    second = to_lanes(jnp.sum(tgt * tgt, axis=1, keepdims=True) - (1.0 / ALPHA) * lse_t)
    picked = first[:, 0:count]
    for i in range(1, rep):
        picked = jnp.where(me % rep == i, first[:, i * count : (i + 1) * count], picked)
    out_ref[0:1, 0:count] = picked
    out_ref[1:2, 0:count] = second[:, 0:count]


def solution(mesh):
    blk_n, grp_n = mesh.shape["blk"], mesh.shape["grp"]
    n_dev = blk_n * grp_n

    def per_device(source, target, source_mass, target_mass):
        count, width = source.shape
        points = n_dev * count
        part = min(4, blk_n)
        while part < blk_n and (points // part) * points * 4 > BUDGET:
            part *= 2
        nj = points // part
        t_dev = n_dev // part
        chunks = points // LANES
        wide = count + SUB
        f32 = jnp.float32
        vmem = pl.BlockSpec(memory_space=pltpu.VMEM)
        dma = pltpu.SemaphoreType.DMA
        out = pl.pallas_call(
            functools.partial(kernel, blk_n, grp_n, part, count),
            out_shape=jax.ShapeDtypeStruct((2, count), f32),
            in_specs=[vmem] * 4,
            out_specs=vmem,
            scratch_shapes=[
                pltpu.VMEM((n_dev, wide, width), f32),
                pltpu.VMEM((t_dev, wide, width), f32),
                pltpu.VMEM((wide, width), f32),
                pltpu.VMEM((wide, width), f32),
                pltpu.VMEM((chunks, nj, LANES), f32),
                pltpu.VMEM((nj, width), f32),
                pltpu.VMEM((nj, LANES), f32),
                pltpu.VMEM((chunks, LANES), f32),
                pltpu.VMEM((chunks, LANES), f32),
                pltpu.VMEM((nj, LANES), f32),
                pltpu.VMEM((2, part, chunks, LANES), f32),
                dma((n_dev,)), dma((n_dev,)),
                dma((t_dev,)), dma((t_dev,)),
                dma((2, part)), dma((2, part)),
            ],
            compiler_params=pltpu.CompilerParams(
                collective_id=0, has_side_effects=True, vmem_limit_bytes=62 * 2**20),
        )(source, target, source_mass.reshape(1, count), target_mass.reshape(1, count))
        return out[0], out[1]

    both = P(("blk", "grp"))
    return jax.shard_map(
        per_device,
        mesh=mesh,
        in_specs=(P(("blk", "grp"), None), P(("blk", "grp"), None), both, both),
        out_specs=(both, both),
        check_vma=False,
    )
```

time: 505 us -> 98.1 us (0.19)
  blocking collectives: 468 us -> 0 us
  Pallas kernels: 0 us -> 96 us
  local copies, waits for them, and re-layouts: 21.5 us -> 1.25 us
  other arithmetic: 8.35 us -> 0 us
    all_gather x36 -> x0, blocking collectives: 315 us -> none  [the longest x32 269 us: combined_all(): pieces = jax.tree.map(lambda part: lax.all_gather(part, axis), value)]
    unnamed x16 -> x0, blocking collectives: 153 us -> none
    pallas_call x0 -> x1, Pallas kernels: none -> 96 us  [per_device(): pl.pallas_call(functools.partial(kernel, blk_n, grp_n, part, count), out_...]
    slice x81 -> x0, local copies, waits for them, and re-layouts: 10.9 us -> none  [the longest x49 10.8 us: combined_all(): head = jax.tree.map(lambda part: part[0], pieces)]
    unnamed x111 -> x0, local copies, waits for them, and re-layouts: 9 us -> none
where the time goes in v1:
time: 98.1 us; the launch traced here: 97.9 us
  Pallas kernels  96 us (98%)
  local copies, waits for them, and re-layouts  1.25 us (1%)
    pallas_call x1, Pallas kernels, per_device(): pl.pallas_call(functools.partial(kernel, blk_n, grp_n, part, count), out_...  96 us

profile of v1, /device:TPU:0, one launch (start us, length us, event | category | flops | bytes accessed | tf_op | source)
XLA Modules:
  0.0 97.9 jit_solution(2755546994872134591)
XLA Ops:
  0.6 96.0 %shard_map.59 = f32[2,64]{1,0:T(2,128)} custom-call(f32[64,128]{1,0:T(8,128)} %src_ref.1, f32[64,128]{1,0:T(8,128)} %tgt_ref.1, f32[1,64]{1,0:T(1,128)} %bitcast.6, f32[1,64]{1,0:T(1,128)} %bitcast.7), custom_call_target="tpu_custom_call" | custom-call | tf_op jit(solution)/shard_map/pallas_call | solution.py:229
  96.6 1.3 %slice_bitcast_fusion = (f32[64]{0:T(128)}, f32[64]{0:T(128)}) fusion(f32[2,64]{1,0:T(2,128)} %shard_map.59), kind=kLoop, calls=%fused_computation | loop fusion | bytes 1024 | tf_op jit(solution)/shard_map/squeeze | solution.py:253

commit v2 on v1

--- a/solution.py
+++ b/solution.py
@@ -14,6 +14,7 @@
 ALPHA = LOG2E / eps
 LANES = 128
 SUB = 8
+OCT = 8
 MESH = pl.DeviceIdType.MESH
 BUDGET = 36 * 2**20
 
@@ -35,7 +36,7 @@
 
 def kernel(blk_n, grp_n, part, count, src_ref, tgt_ref, smass_ref, tmass_ref, out_ref,
            src_all, tgt_all, spack, tpack, cost, tcat, u, v, loga, logb, part_lse,
-           s_send, s_recv, t_send, t_recv, x_send, x_recv):
+           s_send, f_send, s_recv, t_send, t_recv, x_send, x_recv):
     n_dev = blk_n * grp_n
     rep = LANES // count
     chunks = n_dev // rep
@@ -47,14 +48,35 @@
     q, p = b // part, b % part
     mine_t = q * grp_n + g
 
+    peers = n_dev // OCT
+    z, low = (b // OCT) * grp_n + g, b % OCT
+
+    def flip(i, bit):
+        return i + bit * (1 - 2 * ((i // bit) % 2))
+
+    def place(step, bits):
+        peer = lax.rem(z + step, peers)
+        home = low
+        for bit in (1, 2, 4):
+            if bits & bit:
+                home = flip(home, bit)
+        return ((peer // grp_n) * OCT + home) * grp_n + peer % grp_n
+
     barrier = pltpu.get_barrier_semaphore()
 
     def greet(step, _):
-        other = lax.rem(me + step, n_dev)
+        other = place(step, 0)
         pl.semaphore_signal(barrier, inc=1, device_id=(other // grp_n, other % grp_n), device_id_type=MESH)
         return 0
 
-    lax.fori_loop(1, n_dev, greet, 0)
+    lax.fori_loop(1, peers, greet, 0)
+
+    def greet_part(step, _):
+        other = q * part + lax.rem(p + step, part)
+        pl.semaphore_signal(barrier, inc=1, device_id=(other, g), device_id_type=MESH)
+        return 0
+
+    lax.fori_loop(1, part, greet_part, 0)
 
     lane = lax.broadcasted_iota(jnp.int32, (1, LANES), 1)
     here = lane // count == me % rep
@@ -69,7 +91,7 @@
     pack(tgt_ref, tmass_ref, tpack, 1.0)
     src_all[pl.ds(me, 1)] = spack[...][None]
     tgt_all[pl.ds(mine_t, 1)] = tpack[...][None]
-    pl.semaphore_wait(barrier, n_dev - 1)
+    pl.semaphore_wait(barrier, peers + part - 2)
 
     def tgt_copy(slot, r, sem_slot):
         return pltpu.make_async_remote_copy(
@@ -77,19 +99,27 @@
             send_sem=t_send.at[r], recv_sem=t_recv.at[sem_slot],
             device_id=((r // grp_n) * part + p, r % grp_n), device_id_type=MESH)
 
-    def src_copy(slot, d):
+    def src_copy(slot, d, step):
         return pltpu.make_async_remote_copy(
             src_ref=spack, dst_ref=src_all.at[slot],
-            send_sem=s_send.at[d], recv_sem=s_recv.at[slot],
+            send_sem=s_send.at[step], recv_sem=s_recv.at[slot],
             device_id=(d // grp_n, d % grp_n), device_id_type=MESH)
 
+    def push(slot, way):
+        return pltpu.make_async_remote_copy(
+            src_ref=src_all.at[slot], dst_ref=src_all.at[slot],
+            send_sem=f_send.at[way, slot], recv_sem=s_recv.at[slot],
+            device_id=(flip(b, 2 ** way), g), device_id_type=MESH)
+
+    def arrive(slot):
+        src_copy(slot, me, 0).wait_recv()
+
     def send_t(step, _):
-        r = lax.rem(mine_t + step, t_dev)
-        tgt_copy(mine_t, r, mine_t).start()
+        tgt_copy(mine_t, lax.rem(mine_t + step, t_dev), mine_t).start()
         return 0
 
     def send_s(step, _):
-        src_copy(me, lax.rem(me + step, n_dev)).start()
+        src_copy(me, place(step, 0), step).start()
         return 0
 
     def wait_t(step, _):
@@ -98,14 +128,43 @@
         tgt_copy(r, r, r).wait_recv()
         return 0
 
-    def wait_s(step, _):
-        d = lax.rem(me + step, n_dev)
-        src_copy(me, d).wait_send()
-        src_copy(d, d).wait_recv()
-        return 0
-
+    def make_cost(k):
+        pieces = [src_all[k * rep + i, 0:count, :] for i in range(rep)]
+        masses = sum(src_all[k * rep + i, count : count + 1, :] for i in range(rep))
+        loga[pl.ds(k, 1), :] = masses
+        cost[k] = lax.dot_general(
+            tcat[...], jnp.concatenate(pieces, axis=0), (((1,), (1,)), ((), ())),
+            precision=lax.Precision.HIGHEST, preferred_element_type=jnp.float32)
+
+    def costs(bits):
+        home = low
+        for bit in (1, 2, 4):
+            if bits & bit:
+                home = flip(home, bit)
+        per = grp_n // rep
+
+        def one(i, _):
+            make_cost(((i // per) * OCT + home) * per + i % per)
+            return 0
+
+        lax.fori_loop(0, peers // rep, one, 0)
+
+    for way in range(3):
+        push(me, way).start()
+    lax.fori_loop(1, peers, send_s, 0)
     lax.fori_loop(1, t_dev, send_t, 0)
-    lax.fori_loop(1, n_dev, send_s, 0)
+
+    def relay(bits, ways):
+        def go(step, _):
+            slot = place(step, bits)
+            arrive(slot)
+            for way in ways:
+                push(slot, way).start()
+            return 0
+        return go
+
+    half = peers // 2
+    lax.fori_loop(1, peers, relay(0, (1, 2, 0)), 0)
     lax.fori_loop(1, t_dev, wait_t, 0)
 
     eye = (lax.broadcasted_iota(jnp.int32, (count, LANES), 1) % count
@@ -119,18 +178,37 @@
         logb[rows, :] = jnp.broadcast_to(mass, (count, LANES))
         u[rows, :] = jnp.broadcast_to(mass - ALPHA * square, (count, LANES))
 
-    lax.fori_loop(1, n_dev, wait_s, 0)
-
-    def make_cost(k, _):
-        pieces = [src_all[k * rep + i, 0:count, :] for i in range(rep)]
-        masses = sum(src_all[k * rep + i, count : count + 1, :] for i in range(rep))
-        loga[pl.ds(k, 1), :] = masses
-        cost[k] = lax.dot_general(
-            tcat[...], jnp.concatenate(pieces, axis=0), (((1,), (1,)), ((), ())),
-            precision=lax.Precision.HIGHEST, preferred_element_type=jnp.float32)
-        return 0
-
-    lax.fori_loop(0, chunks, make_cost, 0)
+    lax.fori_loop(0, half, relay(2, (2, 0)), 0)
+    lax.fori_loop(0, half, relay(4, (0,)), 0)
+    lax.fori_loop(half, peers, relay(4, (1, 0)), 0)
+    lax.fori_loop(half, peers, relay(2, (0,)), 0)
+    costs(0)
+    costs(2)
+    costs(4)
+    lax.fori_loop(0, peers, relay(6, (0,)), 0)
+    costs(6)
+    for bits in (1, 3, 5, 7):
+        lax.fori_loop(0, peers, relay(bits, ()), 0)
+        costs(bits)
+
+    def sent_s(step, _):
+        src_copy(me, place(step, 0), step).wait_send()
+        return 0
+
+    def sent(bits, ways):
+        def go(step, _):
+            for way in ways:
+                push(place(step, bits), way).wait_send()
+            return 0
+        return go
+
+    lax.fori_loop(1, peers, sent_s, 0)
+    lax.fori_loop(0, peers, sent(0, (0, 1, 2)), 0)
+    lax.fori_loop(0, half, sent(2, (2, 0)), 0)
+    lax.fori_loop(0, half, sent(4, (0,)), 0)
+    lax.fori_loop(half, peers, sent(4, (1, 0)), 0)
+    lax.fori_loop(half, peers, sent(2, (0,)), 0)
+    lax.fori_loop(0, peers, sent(6, (0,)), 0)
 
     rows_at_once = min(nj, 128)
 
@@ -216,7 +294,7 @@
     def per_device(source, target, source_mass, target_mass):
         count, width = source.shape
         points = n_dev * count
-        part = min(4, blk_n)
+        part = OCT
         while part < blk_n and (points // part) * points * 4 > BUDGET:
             part *= 2
         nj = points // part
@@ -243,7 +321,7 @@
                 pltpu.VMEM((chunks, LANES), f32),
                 pltpu.VMEM((nj, LANES), f32),
                 pltpu.VMEM((2, part, chunks, LANES), f32),
-                dma((n_dev,)), dma((n_dev,)),
+                dma((n_dev // OCT,)), dma((3, n_dev)), dma((n_dev,)),
                 dma((t_dev,)), dma((t_dev,)),
                 dma((2, part)), dma((2, part)),
             ],

time: 98.1 us -> 68.3 us (0.70)
  Pallas kernels: 96 us -> 66.2 us
    pallas_call x1, Pallas kernels: 96 us -> 66.2 us  [per_device(): pl.pallas_call(functools.partial(kernel, blk_n, grp_n, part, count), out_...]
where the time goes in v2:
time: 68.3 us; the launch traced here: 68.1 us
  Pallas kernels  66.2 us (97%)
  local copies, waits for them, and re-layouts  1.25 us (2%)
    pallas_call x1, Pallas kernels, per_device(): pl.pallas_call(functools.partial(kernel, blk_n, grp_n, part, count), out_...  66.2 us

profile of v2, /device:TPU:0, one launch (start us, length us, event | category | flops | bytes accessed | tf_op | source)
XLA Modules:
  0.0 68.1 jit_solution(6597561118267630546)
XLA Ops:
  0.6 66.2 %shard_map.59 = f32[2,64]{1,0:T(2,128)} custom-call(f32[64,128]{1,0:T(8,128)} %src_ref.1, f32[64,128]{1,0:T(8,128)} %tgt_ref.1, f32[1,64]{1,0:T(1,128)} %bitcast.6, f32[1,64]{1,0:T(1,128)} %bitcast.7), custom_call_target="tpu_custom_call" | custom-call | tf_op jit(solution)/shard_map/pallas_call | solution.py:307
  66.8 1.3 %slice_bitcast_fusion = (f32[64]{0:T(128)}, f32[64]{0:T(128)}) fusion(f32[2,64]{1,0:T(2,128)} %shard_map.59), kind=kLoop, calls=%fused_computation | loop fusion | bytes 1024 | tf_op jit(solution)/shard_map/squeeze | solution.py:331

commit v3 on v2

--- a/solution.py
+++ b/solution.py
@@ -15,6 +15,9 @@
 LANES = 128
 SUB = 8
 OCT = 8
+PIECES = 2
+UNIT = 4
+GROUPS = 32
 MESH = pl.DeviceIdType.MESH
 BUDGET = 36 * 2**20
 
@@ -24,7 +27,7 @@
 
 
 def log2(x):
-    return jnp.log(x) * LOG2E
+    return jnp.log2(x)
 
 
 def lse_blocks(pairs):
@@ -34,8 +37,8 @@
     return top, sum(s * exp2(m - top) for m, s in pairs)
 
 
-def kernel(blk_n, grp_n, part, count, src_ref, tgt_ref, smass_ref, tmass_ref, out_ref,
-           src_all, tgt_all, spack, tpack, cost, tcat, u, v, loga, logb, part_lse,
+def kernel(blk_n, grp_n, part, count, pieces, src_ref, tgt_ref, smass_ref, tmass_ref, out_ref,
+           src_all, tgt_all, spack, tpack, cost, tcat, u, v, loga, logb, part_lse, piece_top, piece_sum,
            s_send, f_send, s_recv, t_send, t_recv, x_send, x_recv):
     n_dev = blk_n * grp_n
     rep = LANES // count
@@ -129,11 +132,11 @@
         return 0
 
     def make_cost(k):
-        pieces = [src_all[k * rep + i, 0:count, :] for i in range(rep)]
+        blocks = [src_all[k * rep + i, 0:count, :] for i in range(rep)]
         masses = sum(src_all[k * rep + i, count : count + 1, :] for i in range(rep))
         loga[pl.ds(k, 1), :] = masses
         cost[k] = lax.dot_general(
-            tcat[...], jnp.concatenate(pieces, axis=0), (((1,), (1,)), ((), ())),
+            tcat[...], jnp.concatenate(blocks, axis=0), (((1,), (1,)), ((), ())),
             precision=lax.Precision.HIGHEST, preferred_element_type=jnp.float32)
 
     def costs(bits):
@@ -211,60 +214,82 @@
     lax.fori_loop(0, peers, sent(6, (0,)), 0)
 
     rows_at_once = min(nj, 128)
-
-    def source_chunk(slot, k):
-        pairs = []
-        for r in range(0, nj, rows_at_once):
-            x = cost[k, r : r + rows_at_once, :] + u[r : r + rows_at_once, :]
-            x = x.reshape(rows_at_once // SUB, SUB, LANES)
-            m = jnp.max(x, axis=0)
-            pairs.append((m, jnp.sum(exp2(x - m[None]), axis=0)))
-        m, s = lse_blocks(pairs)
-        top = jnp.max(m, axis=0, keepdims=True)
-        total = jnp.sum(s * exp2(m - top), axis=0, keepdims=True)
-        part_lse[slot, p, pl.ds(k, 1), :] = top + log2(total)
-
-    groups = math.gcd(nj // SUB, 8)
-
-    def target_rows(i, _):
+    size = chunks // pieces
+    unit = math.gcd(size, UNIT)
+
+    def source_unit(slot, c, k0):
+        tops, totals = [], []
+        for h in range(unit):
+            pairs = []
+            for r in range(0, nj, rows_at_once):
+                x = cost[c * size + k0 + h, r : r + rows_at_once, :] + u[r : r + rows_at_once, :]
+                x = x.reshape(rows_at_once // SUB, SUB, LANES)
+                m = jnp.max(x, axis=0)
+                pairs.append((m, jnp.sum(exp2(x - m[None]), axis=0)))
+            m, s = lse_blocks(pairs)
+            top = jnp.max(m, axis=0, keepdims=True)
+            tops.append(top)
+            totals.append(jnp.sum(s * exp2(m - top), axis=0, keepdims=True))
+        part_lse[slot, c, p, pl.ds(k0, unit), :] = (
+            jnp.concatenate(tops, axis=0) + log2(jnp.concatenate(totals, axis=0)))
+
+    groups = math.gcd(nj // SUB, GROUPS)
+
+    def target_rows(c, i):
         for h in range(groups):
             rows = pl.ds(pl.multiple_of((i * groups + h) * SUB, SUB), SUB)
             pairs = []
-            for k0 in range(0, chunks, 16):
-                x = [cost[k, rows, :] + v[k : k + 1, :] for k in range(k0, min(k0 + 16, chunks))]
+            for k0 in range(c * size, (c + 1) * size, 16):
+                x = [cost[k, rows, :] + v[k : k + 1, :] for k in range(k0, min(k0 + 16, (c + 1) * size))]
                 m = functools.reduce(jnp.maximum, x)
                 pairs.append((m, sum(exp2(y - m) for y in x)))
             m, s = lse_blocks(pairs)
+            if c < pieces - 1:
+                piece_top[c, rows, :] = m
+                piece_sum[c, rows, :] = s
+                continue
+            m, s = lse_blocks([(m, s)] + [(piece_top[i2, rows, :], piece_sum[i2, rows, :]) for i2 in range(c)])
             top = jnp.max(m, axis=1, keepdims=True)
             total = jnp.sum(s * exp2(m - top), axis=1, keepdims=True)
             u[rows, :] = logb[rows, :] - (top + log2(total))
-        return 0
-
-    def swap(slot, writer, other, sem_at):
+
+    def swap(slot, c, writer, other, sem_at):
         return pltpu.make_async_remote_copy(
-            src_ref=part_lse.at[slot, p], dst_ref=part_lse.at[slot, writer],
-            send_sem=x_send.at[slot, other], recv_sem=x_recv.at[slot, sem_at],
+            src_ref=part_lse.at[slot, c, p], dst_ref=part_lse.at[slot, c, writer],
+            send_sem=x_send.at[slot, c, other], recv_sem=x_recv.at[slot, c, sem_at],
             device_id=(q * part + other, g), device_id_type=MESH)
 
     def iteration(t, _):
         slot = lax.rem(t, 2)
 
-        def one(k, _):
-            source_chunk(slot, k)
-            return 0
-
-        lax.fori_loop(0, chunks, one, 0)
-        for step in range(1, part):
-            other = lax.rem(p + step, part)
-            swap(slot, p, other, p).start()
-        for step in range(1, part):
-            other = lax.rem(p + step, part)
-            swap(slot, p, other, p).wait_send()
-            swap(slot, other, other, other).wait_recv()
-        parts = [part_lse[slot, i] for i in range(part)]
-        top = functools.reduce(jnp.maximum, parts)
-        v[...] = loga[...] - (top + log2(sum(exp2(y - top) for y in parts)))
-        lax.fori_loop(0, nj // (SUB * groups), target_rows, 0)
+        for c in range(pieces):
+            def one(i, _):
+                source_unit(slot, c, i * unit)
+                return 0
+
+            if size == unit:
+                source_unit(slot, c, 0)
+            else:
+                lax.fori_loop(0, size // unit, one, 0)
+            for step in range(1, part):
+                swap(slot, c, p, lax.rem(p + step, part), p).start()
+        for c in range(pieces):
+            for step in range(1, part):
+                other = lax.rem(p + step, part)
+                swap(slot, c, other, other, other).wait_recv()
+            parts = [part_lse[slot, c, i] for i in range(part)]
+            top = functools.reduce(jnp.maximum, parts)
+            rows = slice(c * size, (c + 1) * size)
+            v[rows, :] = loga[rows, :] - (top + log2(sum(exp2(y - top) for y in parts)))
+
+            def two(i, _):
+                target_rows(c, i)
+                return 0
+
+            lax.fori_loop(0, nj // (SUB * groups), two, 0)
+        for c in range(pieces):
+            for step in range(1, part):
+                swap(slot, c, p, lax.rem(p + step, part), p).wait_send()
         return 0
 
     lax.fori_loop(0, ITERS, iteration, 0)
@@ -300,12 +325,13 @@
         nj = points // part
         t_dev = n_dev // part
         chunks = points // LANES
+        pieces = math.gcd(chunks, PIECES)
         wide = count + SUB
         f32 = jnp.float32
         vmem = pl.BlockSpec(memory_space=pltpu.VMEM)
         dma = pltpu.SemaphoreType.DMA
         out = pl.pallas_call(
-            functools.partial(kernel, blk_n, grp_n, part, count),
+            functools.partial(kernel, blk_n, grp_n, part, count, pieces),
             out_shape=jax.ShapeDtypeStruct((2, count), f32),
             in_specs=[vmem] * 4,
             out_specs=vmem,
@@ -320,10 +346,12 @@
                 pltpu.VMEM((chunks, LANES), f32),
                 pltpu.VMEM((chunks, LANES), f32),
                 pltpu.VMEM((nj, LANES), f32),
-                pltpu.VMEM((2, part, chunks, LANES), f32),
+                pltpu.VMEM((2, pieces, part, chunks // pieces, LANES), f32),
+                pltpu.VMEM((pieces, nj, LANES), f32),
+                pltpu.VMEM((pieces, nj, LANES), f32),
                 dma((n_dev // OCT,)), dma((3, n_dev)), dma((n_dev,)),
                 dma((t_dev,)), dma((t_dev,)),
-                dma((2, part)), dma((2, part)),
+                dma((2, pieces, part)), dma((2, pieces, part)),
             ],
             compiler_params=pltpu.CompilerParams(
                 collective_id=0, has_side_effects=True, vmem_limit_bytes=62 * 2**20),

time: 68.3 us -> 59.8 us (0.88)
  Pallas kernels: 66.2 us -> 57.7 us
    pallas_call x1, Pallas kernels: 66.2 us -> 57.7 us  [per_device(): pl.pallas_call(functools.partial(kernel, blk_n, grp_n, part, count, piece...]
where the time goes in v3:
time: 59.8 us; the launch traced here: 59.6 us
  Pallas kernels  57.7 us (96%)
  local copies, waits for them, and re-layouts  1.25 us (2%)
  between operations  0.64 us (1%)
    pallas_call x1, Pallas kernels, per_device(): pl.pallas_call(functools.partial(kernel, blk_n, grp_n, part, count, piece...  57.7 us
    squeeze x1, local copies, waits for them, and re-layouts, per_device(): return (out[0], out[1])  1.25 us

profile of v3, /device:TPU:0, one launch (start us, length us, event | category | flops | bytes accessed | tf_op | source)
XLA Modules:
  0.0 59.6 jit_solution(18015907910864778505)
XLA Ops:
  0.6 57.7 %shard_map.59 = f32[2,64]{1,0:T(2,128)} custom-call(f32[64,128]{1,0:T(8,128)} %src_ref.1, f32[64,128]{1,0:T(8,128)} %tgt_ref.1, f32[1,64]{1,0:T(1,128)} %bitcast.6, f32[1,64]{1,0:T(1,128)} %bitcast.7), custom_call_target="tpu_custom_call" | custom-call | tf_op jit(solution)/shard_map/pallas_call | solution.py:333
  58.3 1.3 %slice_bitcast_fusion = (f32[64]{0:T(128)}, f32[64]{0:T(128)}) fusion(f32[2,64]{1,0:T(2,128)} %shard_map.59), kind=kLoop, calls=%fused_computation | loop fusion | bytes 1024 | tf_op jit(solution)/shard_map/squeeze | solution.py:359
